TPU v7x, 32 devices: a whole 2x2x4 slice. The times are simulated.
32 devices in a mesh: groups: 2 (over y), inner: 4 (over z), outer: 2 (over x), head: 2 (over core).
Axes of the slice: x: 2, y: 2, z: 4, core: 2. Of those that a mesh axis runs over, the one named last changes fastest.
Arguments:
- queries: bfloat16 [4, 512, 8, 128], P(('groups', 'outer'), 'inner', 'head'), parts along dimension 0, may hold values from -112 to 112
- keys: bfloat16 [4, 512, 128], P(('groups', 'outer'), 'inner'), parts along dimension 0, may hold values from -4 to 4
- values: bfloat16 [4, 512, 128], P(('groups', 'outer'), 'inner'), parts along dimension 0, may hold values from -6 to 6
- out: bfloat16 [4, 512, 8, 128], P(('groups', 'outer'), 'inner', 'head'), parts along dimension 0, may hold values from -6 to 6, as said below
- log_total: float32 [4, 8, 512], P(('groups', 'outer'), 'head', 'inner'), parts along dimension 0, as said below
- d_out: bfloat16 [4, 512, 8, 128], P(('groups', 'outer'), 'inner', 'head'), parts along dimension 0, may hold values from -6 to 6
- span_order: int32 [4, 8], P(('groups', 'outer')), parts along dimension 0, may hold values from 0 to 7, as said below
Outputs:
- grad_queries: bfloat16 [4, 512, 8, 128], P(('groups', 'outer'), 'inner', 'head'), parts along dimension 0
- grad_keys: bfloat16 [4, 512, 128], P(('groups', 'outer'), 'inner'), parts along dimension 0
- grad_values: bfloat16 [4, 512, 128], P(('groups', 'outer'), 'inner'), parts along dimension 0
There are 2 independent parts, one for each index of `groups`. A program takes and returns all parts, laid end to end along the dimension named above; each array names one. Nothing has to cross between parts.
Inputs may be any that keep to these rules, and one draw needn't show every extreme that they name: `span_order`: each row is a permutation of 0 to 7. `out`: the causal softmax attention output of queries, keys and values in the order given by span_order, rounded to bfloat16. `log_total`: the log of the causal softmax total of each query row and head for the same inputs.
All inputs are finite; a program needn't handle non-finite values.
Results may differ from a plain program's by a relative error of at most 0.0054.
Values may be sent and summed in bfloat16 or wider, within the bound.
A program may use at most 64 MiB of HBM per device.

v0:
```python
import math

import jax
import jax.numpy as jnp
from jax import lax
from jax.sharding import PartitionSpec as P


def shifted(block, axis, distance):
    devices = range(lax.axis_size(axis))
    route = [((i - distance) % len(devices), i) for i in devices]
    return lax.ppermute(block, axis, route)


def row_positions(block_order, start, count, tok_rows):
    rows = start + jnp.arange(count, dtype=jnp.int32)
    owner = rows // tok_rows
    offset = rows % tok_rows
    half_rows = tok_rows // 2
    slot_index = 2 * owner + offset // half_rows
    table = jnp.arange(block_order.shape[0], dtype=jnp.int32)
    span = jnp.sum(
        jnp.where(slot_index[:, None] == table[None, :], block_order[None, :], 0), axis=1
    )
    return span * half_rows + offset % half_rows


def block_grads(operands):
    query_rows, grad_rows, total_rows, delta_rows, query_pos, key_rows, value_rows, key_pos = (
        operands
    )
    softmax_scale = 1.0 / math.sqrt(key_rows.shape[1])
    visible = key_pos[None, :] <= query_pos[:, None]
    scores = (
        jnp.einsum("thd,ud->htu", query_rows, key_rows, preferred_element_type=jnp.float32)
        * softmax_scale
    )
    probs = jnp.exp(jnp.where(visible[None], scores - total_rows[:, :, None], -jnp.inf))
    grad_probs = jnp.einsum(
        "thd,ud->htu", grad_rows, value_rows, preferred_element_type=jnp.float32
    )
    grad_scores = (probs * (grad_probs - delta_rows[:, :, None]) * softmax_scale).astype(
        jnp.bfloat16
    )
    probs_half = probs.astype(jnp.bfloat16)
    query_grad = jnp.einsum(
        "htu,ud->thd", grad_scores, key_rows, preferred_element_type=jnp.float32
    )
    key_grad = jnp.einsum(
        "htu,thd->ud", grad_scores, query_rows, preferred_element_type=jnp.float32
    )
    value_grad = jnp.einsum(
        "htu,thd->ud", probs_half, grad_rows, preferred_element_type=jnp.float32
    )
    return (query_grad, key_grad, value_grad)


def guarded_grads(operands):
    return block_grads(operands)


def send_key_grads(key_acc, value_acc):
    return shifted((key_acc, value_acc), "inner", 1)


def body(queries, keys, values, out, log_total, d_out, span_order):
    query_rows = queries[0]
    grad_rows = d_out[0]
    key_rows = keys[0]
    value_rows = values[0]
    block_order = span_order[0]
    total_rows = log_total[0]
    tok_rows = key_rows.shape[0]
    cycle_size = lax.axis_size("inner")
    cycle_index = lax.axis_index("inner")
    own_pos = row_positions(block_order, cycle_index * tok_rows, tok_rows, tok_rows)
    delta_rows = jnp.transpose(
        jnp.sum(out[0].astype(jnp.float32) * grad_rows.astype(jnp.float32), axis=-1)
    )
    zero_rows = jnp.zeros(key_rows.shape, jnp.float32)
    zero_queries = jnp.zeros(query_rows.shape, jnp.float32)

    def key_turn(turn_index, state):
        key_block, value_block, query_acc, key_acc, value_acc = state
        owner = (cycle_index - turn_index) % cycle_size
        key_pos = row_positions(block_order, owner * tok_rows, tok_rows, tok_rows)
        query_grad, key_grad, value_grad = guarded_grads(
            (
                query_rows,
                grad_rows,
                total_rows,
                delta_rows,
                own_pos,
                key_block,
                value_block,
                key_pos,
            )
        )
        key_block, value_block = shifted((key_block, value_block), "inner", 1)
        key_acc, value_acc = send_key_grads(key_acc + key_grad, value_acc + value_grad)
        return (key_block, value_block, query_acc + query_grad, key_acc, value_acc)

    state = lax.fori_loop(
        0, cycle_size - 1, key_turn, (key_rows, value_rows, zero_queries, zero_rows, zero_rows)
    )
    key_block, value_block, query_acc, key_acc, value_acc = state
    owner = (cycle_index - (cycle_size - 1)) % cycle_size
    key_pos = row_positions(block_order, owner * tok_rows, tok_rows, tok_rows)
    query_grad, key_grad, value_grad = guarded_grads(
        (query_rows, grad_rows, total_rows, delta_rows, own_pos, key_block, value_block, key_pos)
    )
    query_acc = query_acc + query_grad
    key_acc, value_acc = send_key_grads(key_acc + key_grad, value_acc + value_grad)
    key_total, value_total = lax.psum((key_acc, value_acc), "head")
    grad_queries = query_acc.astype(jnp.bfloat16)[None]
    return (
        grad_queries,
        key_total.astype(jnp.bfloat16)[None],
        value_total.astype(jnp.bfloat16)[None],
    )


def solution(mesh):
    in_specs = (
        P(("groups", "outer"), "inner", "head", None),
        P(("groups", "outer"), "inner", None),
        P(("groups", "outer"), "inner", None),
        P(("groups", "outer"), "inner", "head", None),
        P(("groups", "outer"), "head", "inner"),
        P(("groups", "outer"), "inner", "head", None),
        P(("groups", "outer"), None),
    )
    out_specs = (
        P(("groups", "outer"), "inner", "head", None),
        P(("groups", "outer"), "inner", None),
        P(("groups", "outer"), "inner", None),
    )
    return jax.shard_map(body, mesh=mesh, in_specs=in_specs, out_specs=out_specs, check_vma=False)
```

profile of v0, /device:TPU:0, one launch (start us, length us, event | category | flops | bytes accessed | tf_op | source)
XLA Modules:
  0.0 48.5 jit_solution(17851370137773684488)
XLA Ops:
  0.7 0.8 %copy-done = bf16[1,128,4,128]{3,2,1,0:T(4,128)(2,1)S(1)} copy-done((bf16[1,128,4,128]{3,2,1,0:T(4,128)(2,1)S(1)}, bf16[1,128,4,128]{3,2,1,0:T(4,128)(2,1)}, u32[]{:S(2)}) %copy-start) | copy-done | bytes 131096
  1.5 1.1 %fusion.29 = f32[128,4]{0,1:T(4,128)S(1)} fusion(bf16[1,128,4,128]{3,2,1,0:T(4,128)(2,1)} %param.12, bf16[1,128,4,128]{3,2,1,0:T(4,128)(2,1)S(1)} %copy-done), kind=kLoop, calls=%fused_computation.55 | loop fusion | flops 261632 | bytes 264192 | tf_op jit(solution)/shard_map/reduce_sum | solution.py:78
  2.7 0.6 %copy-done.5 = s32[1,8]{1,0:T(1,128)S(1)} copy-done((s32[1,8]{1,0:T(1,128)S(1)}, s32[1,8]{1,0:T(1,128)}, u32[]{:S(2)}) %copy-start.5) | copy-done | bytes 56
  3.6 0.6 %copy-done.4 = f32[1,4,128]{2,1,0:T(4,128)S(1)} copy-done((f32[1,4,128]{2,1,0:T(4,128)S(1)}, f32[1,4,128]{2,1,0:T(4,128)}, u32[]{:S(2)}) %copy-start.4) | copy-done | bytes 2072
  4.3 32.4 %while.25 = (s32[]{:T(128)}, bf16[128,128]{1,0:T(8,128)(2,1)S(1)}, bf16[128,128]{1,0:T(8,128)(2,1)S(1)}, f32[128,4,128]{2,0,1:T(8,128)S(1)}, f32[128,128]{1,0:T(...) while((s32[]{:T(128)}, bf16[128,128]{1,0:T(8,128)(2,1)S(1)}, ...), condition=%wide.region_4.5_spmd.clone, body=%wide.region_2.4_spmd.clone.sunk | while | flops 84601488 | bytes 3547132 | solution.py:103
  4.3 3.1 %collective-permute-start.1 = (bf16[128,128]{1,0:T(8,128)(2,1)S(1)}, bf16[128,128]{1,0:T(8,128)(2,1)S(1)}, u32[]{:S(2)}, u32[]{:S(2)}) collective-permute-start(bf16[128,128]{1,0:T(8,128)(2,1)S(1)} %copy.47), channel_id=1, source_target_pairs={{12,0},{0,4},{4,8},{8,12},{13,1},{1,5},{5,9},{9,13},{14,2},{2,6},{... | collective-permute-start | bytes 98312 | tf_op jit(solution)/shard_map/while/body/eval_jaxpr/ppermute | solution.py:12
  7.4 1.6 %collective-permute-start = (bf16[128,128]{1,0:T(8,128)(2,1)S(1)}, bf16[128,128]{1,0:T(8,128)(2,1)S(1)}, u32[]{:S(2)}, u32[]{:S(2)}) collective-permute-start(bf16[128,128]{1,0:T(8,128)(2,1)S(1)} %copy.46), channel_id=1, source_target_pairs={{12,0},{0,4},{4,8},{8,12},{13,1},{1,5},{5,9},{9,13},{14,2},{2,6},{... | collective-permute-start | bytes 98312 | tf_op jit(solution)/shard_map/while/body/eval_jaxpr/ppermute | solution.py:12
  9.2 0.2 fusion.71
  9.4 0.2 fusion.72
  9.6 0.2 fusion.74
  9.8 1.6 %collective-permute-start.2 = (f32[128,128]{1,0:T(8,128)S(1)}, f32[128,128]{1,0:T(8,128)S(1)}, u32[]{:S(2)}, u32[]{:S(2)}) collective-permute-start(f32[128,128]{1,0:T(8,128)S(1)} %fusion.74), channel_id=1, source_target_pairs={{12,0},{0,4},{4,8},{8,12},{13,1},{1,5},{5,9},{9,13},{14,2},{2,6},{... | collective-permute-start | bytes 196616 | tf_op jit(solution)/shard_map/while/body/eval_jaxpr/ppermute | solution.py:12
  11.4 0.2 fusion.75
  11.7 0.2 fusion.73
  12.0 1.1 %collective-permute-done = bf16[128,128]{1,0:T(8,128)(2,1)S(1)} collective-permute-done((bf16[128,128]{1,0:T(8,128)(2,1)S(1)}, bf16[128,128]{1,0:T(8,128)(2,1)S(1)}, u32[]{:S(2)}, u32[]{:S(2)}) %collective-permute-start) | collective-permute-done | bytes 32800 | tf_op jit(solution)/shard_map/while/body/eval_jaxpr/ppermute | solution.py:12
  13.1 3.3 %collective-permute-done.2 = f32[128,128]{1,0:T(8,128)S(1)} collective-permute-done((f32[128,128]{1,0:T(8,128)S(1)}, f32[128,128]{1,0:T(8,128)S(1)}, u32[]{:S(2)}, u32[]{:S(2)}) %collective-permute-start.2) | collective-permute-done | bytes 65568 | tf_op jit(solution)/shard_map/while/body/eval_jaxpr/ppermute | solution.py:12
  16.4 1.3 %collective-permute-done.3 = f32[128,128]{1,0:T(8,128)S(1)} collective-permute-done((f32[128,128]{1,0:T(8,128)S(1)}, f32[128,128]{1,0:T(8,128)S(1)}, u32[]{:S(2)}, u32[]{:S(2)}) %collective-permute-start.3) | collective-permute-done | bytes 65568 | tf_op jit(solution)/shard_map/while/body/eval_jaxpr/ppermute | solution.py:12
  18.0 0.2 fusion.71
  18.3 0.2 fusion.72
  18.5 0.2 fusion.74
  18.6 1.5 %collective-permute-start.2 = (f32[128,128]{1,0:T(8,128)S(1)}, f32[128,128]{1,0:T(8,128)S(1)}, u32[]{:S(2)}, u32[]{:S(2)}) collective-permute-start(f32[128,128]{1,0:T(8,128)S(1)} %fusion.74), channel_id=1, source_target_pairs={{12,0},{0,4},{4,8},{8,12},{13,1},{1,5},{5,9},{9,13},{14,2},{2,6},{... | collective-permute-start | bytes 196616 | tf_op jit(solution)/shard_map/while/body/eval_jaxpr/ppermute | solution.py:12
  20.2 0.2 fusion.75
  20.4 3.4 %collective-permute-start.3 = (f32[128,128]{1,0:T(8,128)S(1)}, f32[128,128]{1,0:T(8,128)S(1)}, u32[]{:S(2)}, u32[]{:S(2)}) collective-permute-start(f32[128,128]{1,0:T(8,128)S(1)} %fusion.75), channel_id=1, source_target_pairs={{12,0},{0,4},{4,8},{8,12},{13,1},{1,5},{5,9},{9,13},{14,2},{2,6},{... | collective-permute-start | bytes 196616 | tf_op jit(solution)/shard_map/while/body/eval_jaxpr/ppermute | solution.py:12
  23.8 0.2 fusion.73
  24.1 0.7 %collective-permute-done.2 = f32[128,128]{1,0:T(8,128)S(1)} collective-permute-done((f32[128,128]{1,0:T(8,128)S(1)}, f32[128,128]{1,0:T(8,128)S(1)}, u32[]{:S(2)}, u32[]{:S(2)}) %collective-permute-start.2) | collective-permute-done | bytes 65568 | tf_op jit(solution)/shard_map/while/body/eval_jaxpr/ppermute | solution.py:12
  24.8 1.7 %collective-permute-done.3 = f32[128,128]{1,0:T(8,128)S(1)} collective-permute-done((f32[128,128]{1,0:T(8,128)S(1)}, f32[128,128]{1,0:T(8,128)S(1)}, u32[]{:S(2)}, u32[]{:S(2)}) %collective-permute-start.3) | collective-permute-done | bytes 65568 | tf_op jit(solution)/shard_map/while/body/eval_jaxpr/ppermute | solution.py:12
  26.5 2.1 %collective-permute-start.1 = (bf16[128,128]{1,0:T(8,128)(2,1)S(1)}, bf16[128,128]{1,0:T(8,128)(2,1)S(1)}, u32[]{:S(2)}, u32[]{:S(2)}) collective-permute-start(bf16[128,128]{1,0:T(8,128)(2,1)S(1)} %copy.47), channel_id=1, source_target_pairs={{12,0},{0,4},{4,8},{8,12},{13,1},{1,5},{5,9},{9,13},{14,2},{2,6},{... | collective-permute-start | bytes 98312 | tf_op jit(solution)/shard_map/while/body/eval_jaxpr/ppermute | solution.py:12
  28.5 0.4 collective-permute-start
  29.2 0.2 fusion.71
  29.4 0.2 fusion.72
  29.6 0.2 fusion.74
  29.9 0.2 fusion.75
  30.1 2.5 %collective-permute-start.3 = (f32[128,128]{1,0:T(8,128)S(1)}, f32[128,128]{1,0:T(8,128)S(1)}, u32[]{:S(2)}, u32[]{:S(2)}) collective-permute-start(f32[128,128]{1,0:T(8,128)S(1)} %fusion.75), channel_id=1, source_target_pairs={{12,0},{0,4},{4,8},{8,12},{13,1},{1,5},{5,9},{9,13},{14,2},{2,6},{... | collective-permute-start | bytes 196616 | tf_op jit(solution)/shard_map/while/body/eval_jaxpr/ppermute | solution.py:12
  32.5 0.2 fusion.73
  32.8 1.5 %collective-permute-done = bf16[128,128]{1,0:T(8,128)(2,1)S(1)} collective-permute-done((bf16[128,128]{1,0:T(8,128)(2,1)S(1)}, bf16[128,128]{1,0:T(8,128)(2,1)S(1)}, u32[]{:S(2)}, u32[]{:S(2)}) %collective-permute-start) | collective-permute-done | bytes 32800 | tf_op jit(solution)/shard_map/while/body/eval_jaxpr/ppermute | solution.py:12
  34.3 1.6 %collective-permute-done.2 = f32[128,128]{1,0:T(8,128)S(1)} collective-permute-done((f32[128,128]{1,0:T(8,128)S(1)}, f32[128,128]{1,0:T(8,128)S(1)}, u32[]{:S(2)}, u32[]{:S(2)}) %collective-permute-start.2) | collective-permute-done | bytes 65568 | tf_op jit(solution)/shard_map/while/body/eval_jaxpr/ppermute | solution.py:12
  35.9 0.8 %collective-permute-done.3 = f32[128,128]{1,0:T(8,128)S(1)} collective-permute-done((f32[128,128]{1,0:T(8,128)S(1)}, f32[128,128]{1,0:T(8,128)S(1)}, u32[]{:S(2)}, u32[]{:S(2)}) %collective-permute-start.3) | collective-permute-done | bytes 65568 | tf_op jit(solution)/shard_map/while/body/eval_jaxpr/ppermute | solution.py:12
  36.7 0.2 fusion.19
  36.9 0.2 fusion.24
  37.1 0.2 fusion.27
  37.3 0.6 %collective-permute-start.4 = (f32[128,128]{1,0:T(8,128)S(1)}, f32[128,128]{1,0:T(8,128)S(1)}, u32[]{:S(2)}, u32[]{:S(2)}) collective-permute-start(f32[128,128]{1,0:T(8,128)S(1)} %fusion.27), channel_id=1, source_target_pairs={{12,0},{0,4},{4,8},{8,12},{13,1},{1,5},{5,9},{9,13},{14,2},{2,6},{... | collective-permute-start | bytes 196616 | tf_op jit(solution)/shard_map/ppermute | solution.py:12
  37.9 0.2 fusion.28
  38.1 1.9 %collective-permute-start.5 = (f32[128,128]{1,0:T(8,128)S(1)}, f32[128,128]{1,0:T(8,128)S(1)}, u32[]{:S(2)}, u32[]{:S(2)}) collective-permute-start(f32[128,128]{1,0:T(8,128)S(1)} %fusion.28), channel_id=1, source_target_pairs={{12,0},{0,4},{4,8},{8,12},{13,1},{1,5},{5,9},{9,13},{14,2},{2,6},{... | collective-permute-start | bytes 196616 | tf_op jit(solution)/shard_map/ppermute | solution.py:12
  40.0 0.1 copy.24
  40.2 0.2 fusion.26
  40.4 0.8 %copy.25 = bf16[1,128,4,128]{3,2,1,0:T(4,128)(2,1)} copy(bf16[1,128,4,128]{1,3,2,0:T(8,128)(2,1)S(1)} %fusion.26) | data formatting | bytes 262144
  41.2 2.3 %collective-permute-done.4 = f32[128,128]{1,0:T(8,128)S(1)} collective-permute-done((f32[128,128]{1,0:T(8,128)S(1)}, f32[128,128]{1,0:T(8,128)S(1)}, u32[]{:S(2)}, u32[]{:S(2)}) %collective-permute-start.4) | collective-permute-done | bytes 65568 | tf_op jit(solution)/shard_map/ppermute | solution.py:12
  43.4 0.7 %collective-permute-done.5 = f32[128,128]{1,0:T(8,128)S(1)} collective-permute-done((f32[128,128]{1,0:T(8,128)S(1)}, f32[128,128]{1,0:T(8,128)S(1)}, u32[]{:S(2)}, u32[]{:S(2)}) %collective-permute-start.5) | collective-permute-done | bytes 65568 | tf_op jit(solution)/shard_map/ppermute | solution.py:12
  44.2 4.4 %all-reduce.2 = (bf16[128,128]{1,0:T(8,128)(2,1)}, bf16[128,128]{1,0:T(8,128)(2,1)}) all-reduce(f32[128,128]{1,0:T(8,128)S(1)} %collective-permute-done.4, f32[128,128]{1,0:T(8,128)S(1)} %collective-permute-done.5), channel_id=1, replica_groups=mesh['groups'=2,'inner'=4,'outer'=2,'head'=2] {'head'}, use_global_device_ids=true, to_apply=%region_6.7 | all-reduce | flops 32768 | bytes 196608 | tf_op jit(solution)/shard_map/psum | solution.py:114
  (44 shorter events, 1.4 us)
Async XLA Ops:
  0.6 0.9 %copy-start = (bf16[1,128,4,128]{3,2,1,0:T(4,128)(2,1)S(1)}, bf16[1,128,4,128]{3,2,1,0:T(4,128)(2,1)}, u32[]{:S(2)}) copy-start(bf16[1,128,4,128]{3,2,1,0:T(4,128)(2,1)} %param.14) | copy-start | bytes 393220
  1.5 1.1 %copy-start.3 = (bf16[1,128,4,128]{3,2,1,0:T(4,128)(2,1)S(1)}, bf16[1,128,4,128]{3,2,1,0:T(4,128)(2,1)}, u32[]{:S(2)}) copy-start(bf16[1,128,4,128]{3,2,1,0:T(4,128)(2,1)} %param.9) | copy-start | bytes 393220
  2.7 0.7 %copy-start.5 = (s32[1,8]{1,0:T(1,128)S(1)}, s32[1,8]{1,0:T(1,128)}, u32[]{:S(2)}) copy-start(s32[1,8]{1,0:T(1,128)} %param.15) | copy-start | bytes 100
  3.5 0.7 %copy-start.4 = (f32[1,4,128]{2,1,0:T(4,128)S(1)}, f32[1,4,128]{2,1,0:T(4,128)}, u32[]{:S(2)}) copy-start(f32[1,4,128]{2,1,0:T(4,128)} %param.13) | copy-start | bytes 6148
  3.6 0.8 %copy-start.1 = (bf16[1,128,128]{2,1,0:T(8,128)(2,1)S(1)}, bf16[1,128,128]{2,1,0:T(8,128)(2,1)}, u32[]{:S(2)}) copy-start(bf16[1,128,128]{2,1,0:T(8,128)(2,1)} %param.10) | copy-start | bytes 98308
  3.6 0.8 %copy-start.2 = (bf16[1,128,128]{2,1,0:T(8,128)(2,1)S(1)}, bf16[1,128,128]{2,1,0:T(8,128)(2,1)}, u32[]{:S(2)}) copy-start(bf16[1,128,128]{2,1,0:T(8,128)(2,1)} %param.11) | copy-start | bytes 98308
  4.3 7.6 %collective-permute-start.1 = (bf16[128,128]{1,0:T(8,128)(2,1)S(1)}, bf16[128,128]{1,0:T(8,128)(2,1)S(1)}, u32[]{:S(2)}, u32[]{:S(2)}) collective-permute-start(bf16[128,128]{1,0:T(8,128)(2,1)S(1)} %copy.47), channel_id=1, source_target_pairs={{12,0},{0,4},{4,8},{8,12},{13,1},{1,5},{5,9},{9,13},{14,2},{2,6},{... | collective-permute-start | bytes 98312 | tf_op jit(solution)/shard_map/while/body/eval_jaxpr/ppermute | solution.py:12
  7.4 5.7 %collective-permute-start = (bf16[128,128]{1,0:T(8,128)(2,1)S(1)}, bf16[128,128]{1,0:T(8,128)(2,1)S(1)}, u32[]{:S(2)}, u32[]{:S(2)}) collective-permute-start(bf16[128,128]{1,0:T(8,128)(2,1)S(1)} %copy.46), channel_id=1, source_target_pairs={{12,0},{0,4},{4,8},{8,12},{13,1},{1,5},{5,9},{9,13},{14,2},{2,6},{... | collective-permute-start | bytes 98312 | tf_op jit(solution)/shard_map/while/body/eval_jaxpr/ppermute | solution.py:12
  9.8 6.7 %collective-permute-start.2 = (f32[128,128]{1,0:T(8,128)S(1)}, f32[128,128]{1,0:T(8,128)S(1)}, u32[]{:S(2)}, u32[]{:S(2)}) collective-permute-start(f32[128,128]{1,0:T(8,128)S(1)} %fusion.74), channel_id=1, source_target_pairs={{12,0},{0,4},{4,8},{8,12},{13,1},{1,5},{5,9},{9,13},{14,2},{2,6},{... | collective-permute-start | bytes 196616 | tf_op jit(solution)/shard_map/while/body/eval_jaxpr/ppermute | solution.py:12
  11.6 6.1 %collective-permute-start.3 = (f32[128,128]{1,0:T(8,128)S(1)}, f32[128,128]{1,0:T(8,128)S(1)}, u32[]{:S(2)}, u32[]{:S(2)}) collective-permute-start(f32[128,128]{1,0:T(8,128)S(1)} %fusion.75), channel_id=1, source_target_pairs={{12,0},{0,4},{4,8},{8,12},{13,1},{1,5},{5,9},{9,13},{14,2},{2,6},{... | collective-permute-start | bytes 196616 | tf_op jit(solution)/shard_map/while/body/eval_jaxpr/ppermute | solution.py:12
  17.7 6.3 %collective-permute-start.1 = (bf16[128,128]{1,0:T(8,128)(2,1)S(1)}, bf16[128,128]{1,0:T(8,128)(2,1)S(1)}, u32[]{:S(2)}, u32[]{:S(2)}) collective-permute-start(bf16[128,128]{1,0:T(8,128)(2,1)S(1)} %copy.47), channel_id=1, source_target_pairs={{12,0},{0,4},{4,8},{8,12},{13,1},{1,5},{5,9},{9,13},{14,2},{2,6},{... | collective-permute-start | bytes 98312 | tf_op jit(solution)/shard_map/while/body/eval_jaxpr/ppermute | solution.py:12
  17.7 6.3 %collective-permute-start = (bf16[128,128]{1,0:T(8,128)(2,1)S(1)}, bf16[128,128]{1,0:T(8,128)(2,1)S(1)}, u32[]{:S(2)}, u32[]{:S(2)}) collective-permute-start(bf16[128,128]{1,0:T(8,128)(2,1)S(1)} %copy.46), channel_id=1, source_target_pairs={{12,0},{0,4},{4,8},{8,12},{13,1},{1,5},{5,9},{9,13},{14,2},{2,6},{... | collective-permute-start | bytes 98312 | tf_op jit(solution)/shard_map/while/body/eval_jaxpr/ppermute | solution.py:12
  18.6 6.1 %collective-permute-start.2 = (f32[128,128]{1,0:T(8,128)S(1)}, f32[128,128]{1,0:T(8,128)S(1)}, u32[]{:S(2)}, u32[]{:S(2)}) collective-permute-start(f32[128,128]{1,0:T(8,128)S(1)} %fusion.74), channel_id=1, source_target_pairs={{12,0},{0,4},{4,8},{8,12},{13,1},{1,5},{5,9},{9,13},{14,2},{2,6},{... | collective-permute-start | bytes 196616 | tf_op jit(solution)/shard_map/while/body/eval_jaxpr/ppermute | solution.py:12
  20.4 6.1 %collective-permute-start.3 = (f32[128,128]{1,0:T(8,128)S(1)}, f32[128,128]{1,0:T(8,128)S(1)}, u32[]{:S(2)}, u32[]{:S(2)}) collective-permute-start(f32[128,128]{1,0:T(8,128)S(1)} %fusion.75), channel_id=1, source_target_pairs={{12,0},{0,4},{4,8},{8,12},{13,1},{1,5},{5,9},{9,13},{14,2},{2,6},{... | collective-permute-start | bytes 196616 | tf_op jit(solution)/shard_map/while/body/eval_jaxpr/ppermute | solution.py:12
  26.5 6.3 %collective-permute-start.1 = (bf16[128,128]{1,0:T(8,128)(2,1)S(1)}, bf16[128,128]{1,0:T(8,128)(2,1)S(1)}, u32[]{:S(2)}, u32[]{:S(2)}) collective-permute-start(bf16[128,128]{1,0:T(8,128)(2,1)S(1)} %copy.47), channel_id=1, source_target_pairs={{12,0},{0,4},{4,8},{8,12},{13,1},{1,5},{5,9},{9,13},{14,2},{2,6},{... | collective-permute-start | bytes 98312 | tf_op jit(solution)/shard_map/while/body/eval_jaxpr/ppermute | solution.py:12
  28.5 5.7 %collective-permute-start = (bf16[128,128]{1,0:T(8,128)(2,1)S(1)}, bf16[128,128]{1,0:T(8,128)(2,1)S(1)}, u32[]{:S(2)}, u32[]{:S(2)}) collective-permute-start(bf16[128,128]{1,0:T(8,128)(2,1)S(1)} %copy.46), channel_id=1, source_target_pairs={{12,0},{0,4},{4,8},{8,12},{13,1},{1,5},{5,9},{9,13},{14,2},{2,6},{... | collective-permute-start | bytes 98312 | tf_op jit(solution)/shard_map/while/body/eval_jaxpr/ppermute | solution.py:12
  29.8 6.1 %collective-permute-start.2 = (f32[128,128]{1,0:T(8,128)S(1)}, f32[128,128]{1,0:T(8,128)S(1)}, u32[]{:S(2)}, u32[]{:S(2)}) collective-permute-start(f32[128,128]{1,0:T(8,128)S(1)} %fusion.74), channel_id=1, source_target_pairs={{12,0},{0,4},{4,8},{8,12},{13,1},{1,5},{5,9},{9,13},{14,2},{2,6},{... | collective-permute-start | bytes 196616 | tf_op jit(solution)/shard_map/while/body/eval_jaxpr/ppermute | solution.py:12
  30.1 6.7 %collective-permute-start.3 = (f32[128,128]{1,0:T(8,128)S(1)}, f32[128,128]{1,0:T(8,128)S(1)}, u32[]{:S(2)}, u32[]{:S(2)}) collective-permute-start(f32[128,128]{1,0:T(8,128)S(1)} %fusion.75), channel_id=1, source_target_pairs={{12,0},{0,4},{4,8},{8,12},{13,1},{1,5},{5,9},{9,13},{14,2},{2,6},{... | collective-permute-start | bytes 196616 | tf_op jit(solution)/shard_map/while/body/eval_jaxpr/ppermute | solution.py:12
  37.3 6.1 %collective-permute-start.4 = (f32[128,128]{1,0:T(8,128)S(1)}, f32[128,128]{1,0:T(8,128)S(1)}, u32[]{:S(2)}, u32[]{:S(2)}) collective-permute-start(f32[128,128]{1,0:T(8,128)S(1)} %fusion.27), channel_id=1, source_target_pairs={{12,0},{0,4},{4,8},{8,12},{13,1},{1,5},{5,9},{9,13},{14,2},{2,6},{... | collective-permute-start | bytes 196616 | tf_op jit(solution)/shard_map/ppermute | solution.py:12
  38.1 6.1 %collective-permute-start.5 = (f32[128,128]{1,0:T(8,128)S(1)}, f32[128,128]{1,0:T(8,128)S(1)}, u32[]{:S(2)}, u32[]{:S(2)}) collective-permute-start(f32[128,128]{1,0:T(8,128)S(1)} %fusion.28), channel_id=1, source_target_pairs={{12,0},{0,4},{4,8},{8,12},{13,1},{1,5},{5,9},{9,13},{14,2},{2,6},{... | collective-permute-start | bytes 196616 | tf_op jit(solution)/shard_map/ppermute | solution.py:12
where the time goes:
time: 48.8 us; the launch traced here: 48.5 us
  starting transfers between devices  19 us (39%)
  waiting for transfers between devices  15.1 us (31%)
  blocking collectives  4.36 us (9%)
  matrix products  3.93 us (8%)
  local copies, waits for them, and re-layouts  3.2 us (7%)
  other arithmetic  1.95 us (4%)
  between operations  0.81 us (2%)
    ppermute x14, starting transfers between devices, shifted(): return lax.ppermute(block, axis, route)  19 us
    ppermute x14, waiting for transfers between devices, shifted(): return lax.ppermute(block, axis, route)  15.1 us
    psum x1, blocking collectives, body(): key_total, value_total = lax.psum((key_acc, value_acc), 'head')  4.36 us
    unnamed x13, local copies, waits for them, and re-layouts  3 us
    reduce_sum x1, other arithmetic, body(): jnp.sum(out[0].astype(jnp.float32) * grad_rows.astype(jnp.float32), axis=-1)  1.08 us
  transfers between devices with their start and end apart: 14, of which 10 were waited for; matrix products, arithmetic and copies ran while one was open for 10% of the time, Pallas kernels for 0%

commit v1 on v0

v1 whole, which is shorter than its diff:
```python
import functools
import math

import jax
import jax.numpy as jnp
from jax import lax
from jax.experimental import pallas as pl
from jax.experimental.pallas import tpu as pltpu
from jax.sharding import PartitionSpec as P

MESH = pl.DeviceIdType.MESH
F32 = jnp.float32
BF16 = jnp.bfloat16
NT = (((1,), (1,)), ((), ()))
TN = (((0,), (0,)), ((), ()))
LOG2E = math.log2(math.e)


def dot(a, b, dims=(((1,), (0,)), ((), ()))):
    return lax.dot_general(a, b, dims, preferred_element_type=F32)


def kernel(
    n,
    heads,
    q_hbm,
    k_hbm,
    v_hbm,
    o_hbm,
    l_hbm,
    g_hbm,
    order,
    dq_hbm,
    dk_hbm,
    dv_hbm,
    qs,
    gs,
    os_,
    ls,
    kv,
    stat,
    ds_all,
    part,
    send_buf,
    recv_buf,
    dq_send,
    dq_recv,
    dq_out,
    fin,
    load_sem,
    pair_send,
    pair_recv,
    kv_send,
    kv_recv,
    grad_send,
    grad_recv,
    out_sem,
):
    me = lax.axis_index("inner")
    core = lax.axis_index("head")
    other = 1 - core
    half, width = kv.shape[2], kv.shape[3]
    rows = qs.shape[1]
    scale = 1.0 / math.sqrt(width)
    partner = {"head": other}

    def at(d):
        return {"inner": lax.rem(me + d, n)}

    barrier = pltpu.get_barrier_semaphore()
    for d in range(1, n):
        pl.semaphore_signal(barrier, inc=1, device_id=at(d), device_id_type=MESH)
    pl.semaphore_signal(barrier, inc=1, device_id=partner, device_id_type=MESH)

    mine = pl.ds(pl.multiple_of(core * half, half), half)
    theirs = pl.ds(pl.multiple_of(other * half, half), half)
    loads = [
        pltpu.make_async_copy(src, dst, load_sem.at[i])
        for i, (src, dst) in enumerate(
            (
                (k_hbm.at[mine], kv.at[0, 0]),
                (v_hbm.at[mine], kv.at[0, 1]),
                (q_hbm, qs.at[0]),
                (g_hbm, gs.at[0]),
                (o_hbm, os_.at[0]),
                (l_hbm, ls.at[0]),
            )
        )
    ]
    for load in loads:
        load.start()

    loads[0].wait()
    loads[1].wait()
    pl.semaphore_wait(barrier, n)
    near = sorted(range(1, n), key=lambda d: (-min(d, n - d), d))
    kv_copies = {}
    for d in near:
        kv_copies[d] = pltpu.make_async_remote_copy(
            src_ref=kv.at[0],
            dst_ref=kv.at[d],
            send_sem=kv_send.at[d],
            recv_sem=kv_recv.at[d],
            device_id=at(d),
            device_id_type=MESH,
        )
        kv_copies[d].start()
    pair_copies = []
    for i, ref in enumerate((qs, gs, os_, ls)):
        loads[2 + i].wait()
        copy = pltpu.make_async_remote_copy(
            src_ref=ref.at[0],
            dst_ref=ref.at[1],
            send_sem=pair_send.at[i],
            recv_sem=pair_recv.at[i],
            device_id=partner,
            device_id_type=MESH,
        )
        copy.start()
        pair_copies.append(copy)

    toks = rows // heads
    col = lax.broadcasted_iota(jnp.int32, (toks, rows), 1)
    spread = jnp.where(
        col // heads == lax.broadcasted_iota(jnp.int32, (toks, rows), 0), 1.0, 0.0
    )
    head_of = lax.broadcasted_iota(jnp.int32, (heads, rows), 1) % heads
    pick = head_of == lax.broadcasted_iota(jnp.int32, (heads, rows), 0)
    ones = jnp.ones((8, width), BF16)

    def stats(i):
        total = jnp.dot(
            ls[i], spread, preferred_element_type=F32, precision=lax.Precision.HIGHEST
        )
        total = jnp.sum(jnp.where(pick, total, 0.0), axis=0, keepdims=True)
        prod = os_[i].astype(F32) * gs[i].astype(F32)
        high = prod.astype(BF16)
        low = (prod - high.astype(F32)).astype(BF16)
        delta = dot(ones, high, NT) + dot(ones, low, NT)
        stat[0:1, i * rows : (i + 1) * rows] = total * LOG2E
        stat[1:2, i * rows : (i + 1) * rows] = delta[0:1]

    stats(0)
    for copy in pair_copies:
        copy.wait_recv()
    stats(1)

    tok = (lax.broadcasted_iota(jnp.int32, (1, rows), 1)) // heads
    span = jnp.where(tok < half, order[2 * me], order[2 * me + 1])
    q_pos = span * half + tok % half
    q_pos = jnp.concatenate([q_pos, q_pos], axis=1)
    key_row = lax.broadcasted_iota(jnp.int32, (half, 1), 0)

    def block(d):
        owner = lax.rem(me + (n - d), n)
        k_pos = order[2 * owner + core] * half + key_row
        visible = k_pos <= q_pos
        queries = qs[...].reshape(2 * rows, width)
        grads = gs[...].reshape(2 * rows, width)
        scores = dot(kv[d, 0], queries, NT)
        grad_probs = dot(kv[d, 1], grads, NT)
        probs = jnp.exp2(
            jnp.where(visible, scores * (scale * LOG2E) - stat[0:1, :], -jnp.inf)
        )
        grad_scores = (probs * (grad_probs - stat[1:2, :]) * scale).astype(BF16)
        ds_all[d] = grad_scores
        return dot(grad_scores, queries), dot(probs.astype(BF16), grads)

    part[0], part[1] = block(0)
    grad_copies = {}
    for d in reversed(near):
        kv_copies[d].wait_recv()
        key_grad, value_grad = block(d)
        send_buf[d, 0] = key_grad.astype(BF16)
        send_buf[d, 1] = value_grad.astype(BF16)
        grad_copies[d] = pltpu.make_async_remote_copy(
            src_ref=send_buf.at[d],
            dst_ref=recv_buf.at[d],
            send_sem=grad_send.at[d],
            recv_sem=grad_recv.at[d],
            device_id=at(n - d),
            device_id_type=MESH,
        )
        grad_copies[d].start()

    def query_grad(i):
        total = None
        for d in range(n):
            term = dot(ds_all[d, :, i * rows : (i + 1) * rows], kv[d, 0], TN)
            total = term if total is None else total + term
        return total

    dq_send[...] = query_grad(1)
    dq_copy = pltpu.make_async_remote_copy(
        src_ref=dq_send,
        dst_ref=dq_recv,
        send_sem=pair_send.at[4],
        recv_sem=pair_recv.at[4],
        device_id=partner,
        device_id_type=MESH,
    )
    dq_copy.start()
    own_grad = query_grad(0)
    dq_copy.wait_recv()
    dq_out[...] = (own_grad + dq_recv[...]).astype(BF16)
    outs = [pltpu.make_async_copy(dq_out, dq_hbm, out_sem.at[0])]
    outs[0].start()

    total = part[...]
    for d in reversed(near):
        grad_copies[d].wait_recv()
        total = total + recv_buf[d].astype(F32)
    fin[0] = total.astype(BF16)
    fin_copy = pltpu.make_async_remote_copy(
        src_ref=fin.at[0],
        dst_ref=fin.at[1],
        send_sem=pair_send.at[5],
        recv_sem=pair_recv.at[5],
        device_id=partner,
        device_id_type=MESH,
    )
    fin_copy.start()
    for i, ref in enumerate((dk_hbm, dv_hbm)):
        outs.append(pltpu.make_async_copy(fin.at[0, i], ref.at[mine], out_sem.at[1 + i]))
        outs[-1].start()
    fin_copy.wait_recv()
    for i, ref in enumerate((dk_hbm, dv_hbm)):
        outs.append(pltpu.make_async_copy(fin.at[1, i], ref.at[theirs], out_sem.at[3 + i]))
        outs[-1].start()
    for d in near:
        kv_copies[d].wait_send()
        grad_copies[d].wait_send()
    for copy in pair_copies + [dq_copy, fin_copy]:
        copy.wait_send()
    for out in outs:
        out.wait()


def body(n, queries, keys, values, out, log_total, d_out, span_order):
    _, toks, heads, width = queries.shape
    rows = toks * heads
    half = toks // 2
    flat = lambda x: x.reshape(rows, width)
    anywhere = pl.BlockSpec(memory_space=pl.ANY)
    dq, dk, dv = pl.pallas_call(
        functools.partial(kernel, n, heads),
        out_shape=(
            jax.ShapeDtypeStruct((rows, width), BF16),
            jax.ShapeDtypeStruct((toks, width), BF16),
            jax.ShapeDtypeStruct((toks, width), BF16),
        ),
        in_specs=[anywhere] * 6 + [pl.BlockSpec(memory_space=pltpu.SMEM)],
        out_specs=(anywhere,) * 3,
        scratch_shapes=[
            pltpu.VMEM((2, rows, width), BF16),
            pltpu.VMEM((2, rows, width), BF16),
            pltpu.VMEM((2, rows, width), BF16),
            pltpu.VMEM((2, heads, toks), F32),
            pltpu.VMEM((n, 2, half, width), BF16),
            pltpu.VMEM((8, 2 * rows), F32),
            pltpu.VMEM((n, half, 2 * rows), BF16),
            pltpu.VMEM((2, half, width), F32),
            pltpu.VMEM((n, 2, half, width), BF16),
            pltpu.VMEM((n, 2, half, width), BF16),
            pltpu.VMEM((rows, width), F32),
            pltpu.VMEM((rows, width), F32),
            pltpu.VMEM((rows, width), BF16),
            pltpu.VMEM((2, 2, half, width), BF16),
            pltpu.SemaphoreType.DMA((6,)),
            pltpu.SemaphoreType.DMA((6,)),
            pltpu.SemaphoreType.DMA((6,)),
            pltpu.SemaphoreType.DMA((n,)),
            pltpu.SemaphoreType.DMA((n,)),
            pltpu.SemaphoreType.DMA((n,)),
            pltpu.SemaphoreType.DMA((n,)),
            pltpu.SemaphoreType.DMA((5,)),
        ],
        compiler_params=pltpu.CompilerParams(collective_id=0, has_side_effects=True),
    )(
        flat(queries),
        keys[0],
        values[0],
        flat(out),
        log_total[0],
        flat(d_out),
        span_order[0],
    )
    return dq.reshape(queries.shape), dk[None], dv[None]


def solution(mesh):
    seq = ("groups", "outer")
    wide = P(seq, "inner", "head", None)
    narrow = P(seq, "inner", None)
    return jax.shard_map(
        functools.partial(body, mesh.shape["inner"]),
        mesh=mesh,
        in_specs=(wide, narrow, narrow, wide, P(seq, "head", "inner"), wide, P(seq, None)),
        out_specs=(wide, narrow, narrow),
        check_vma=False,
    )
```

time: 48.8 us -> 20.3 us (0.42)
  the two profiles are of different devices: /device:TPU:0 before, /device:TPU:1 now
where the time goes in v1:
time: 20.3 us; the launch traced here: 20 us
  Pallas kernels  16.4 us (81%)
  local copies, waits for them, and re-layouts  3 us (15%)
  between operations  0.65 us (3%)
    pallas_call x1, Pallas kernels, body(): pl.pallas_call(functools.partial(kernel, n, heads), out_shape=(jax.ShapeD...  16.4 us
    unnamed x7, local copies, waits for them, and re-layouts  3 us

profile of v1, /device:TPU:1, one launch (start us, length us, event | category | flops | bytes accessed | tf_op | source)
XLA Modules:
  0.0 20.0 jit_solution(12480710085991470771)
XLA Ops:
  0.6 16.4 %shard_map.94 = (bf16[512,128]{1,0:T(8,128)(2,1)}, bf16[128,128]{1,0:T(8,128)(2,1)}, bf16[128,128]{1,0:T(8,128)(2,1)}) custom-call(bf16[512,128]{1,0:T(8,128)(2,1)} %bitcast.11, bf16[128,128]{1,0:T(8,128)(2,1)} %bitcast.14, bf16[128,128]{1,0:T(8,128)(2,1)} %bitcast.15, bf16[512,128]{1,0:T(8,128)(2,1)} %bitcast.12, f32[4,128]{1,0:T(4,128)} %bitcast.18, ...), custom_call_target="tpu_custom_call" | custom-call | tf_op jit(solution)/shard_map/pallas_call | solution.py:245
  17.0 0.0 copy-start.1
  17.0 1.6 %copy.13 = bf16[1,128,4,128]{3,2,1,0:T(4,128)(2,1)} copy(bf16[1,128,4,128]{3,2,1,0:T(4,128)(2,1)} %bitcast.10) | data formatting | bytes 262144
  18.6 0.0 copy-done.1
  18.6 0.0 copy-start
  18.6 0.6 %copy.14 = bf16[1,128,128]{2,1,0:T(8,128)(2,1)} copy(bf16[1,128,128]{2,1,0:T(8,128)(2,1)S(1)} %bitcast.17) | data formatting | bytes 65536
  19.2 0.2 copy-done
  19.4 0.6 %copy.15 = bf16[1,128,128]{2,1,0:T(8,128)(2,1)} copy(bf16[1,128,128]{2,1,0:T(8,128)(2,1)S(1)} %bitcast.16) | data formatting | bytes 65536
Async XLA Ops:
  17.0 1.6 %copy-start.1 = (bf16[128,128]{1,0:T(8,128)(2,1)S(1)}, bf16[128,128]{1,0:T(8,128)(2,1)}, u32[]{:S(2)}) copy-start(bf16[128,128]{1,0:T(8,128)(2,1)} %get-tuple-element.7) | copy-start | bytes 98308
  18.6 0.8 %copy-start = (bf16[128,128]{1,0:T(8,128)(2,1)S(1)}, bf16[128,128]{1,0:T(8,128)(2,1)}, u32[]{:S(2)}) copy-start(bf16[128,128]{1,0:T(8,128)(2,1)} %get-tuple-element.8) | copy-start | bytes 98308

commit v2 on v1

--- a/solution.py
+++ b/solution.py
@@ -30,9 +30,8 @@
     l_hbm,
     g_hbm,
     order,
-    dq_hbm,
-    dk_hbm,
-    dv_hbm,
+    dq_ref,
+    kv_ref,
     qs,
     gs,
     os_,
@@ -45,7 +44,6 @@
     recv_buf,
     dq_send,
     dq_recv,
-    dq_out,
     fin,
     load_sem,
     pair_send,
@@ -54,7 +52,6 @@
     kv_recv,
     grad_send,
     grad_recv,
-    out_sem,
 ):
     me = lax.axis_index("inner")
     core = lax.axis_index("head")
@@ -202,9 +199,7 @@
     dq_copy.start()
     own_grad = query_grad(0)
     dq_copy.wait_recv()
-    dq_out[...] = (own_grad + dq_recv[...]).astype(BF16)
-    outs = [pltpu.make_async_copy(dq_out, dq_hbm, out_sem.at[0])]
-    outs[0].start()
+    dq_ref[...] = (own_grad + dq_recv[...]).astype(BF16)
 
     total = part[...]
     for d in reversed(near):
@@ -220,20 +215,23 @@
         device_id_type=MESH,
     )
     fin_copy.start()
-    for i, ref in enumerate((dk_hbm, dv_hbm)):
-        outs.append(pltpu.make_async_copy(fin.at[0, i], ref.at[mine], out_sem.at[1 + i]))
-        outs[-1].start()
+    kv_ref[:, mine] = fin[0]
     fin_copy.wait_recv()
-    for i, ref in enumerate((dk_hbm, dv_hbm)):
-        outs.append(pltpu.make_async_copy(fin.at[1, i], ref.at[theirs], out_sem.at[3 + i]))
-        outs[-1].start()
+    kv_ref[:, theirs] = fin[1]
     for d in near:
         kv_copies[d].wait_send()
         grad_copies[d].wait_send()
     for copy in pair_copies + [dq_copy, fin_copy]:
         copy.wait_send()
-    for out in outs:
-        out.wait()
+
+
+def store_kernel(dq_ref, kv_ref, dq_hbm, dk_hbm, dv_hbm, sem):
+    pairs = ((dq_ref, dq_hbm), (kv_ref.at[0], dk_hbm), (kv_ref.at[1], dv_hbm))
+    copies = [pltpu.make_async_copy(a, b, sem.at[i]) for i, (a, b) in enumerate(pairs)]
+    for copy in copies:
+        copy.start()
+    for copy in copies:
+        copy.wait()
 
 
 def body(n, queries, keys, values, out, log_total, d_out, span_order):
@@ -241,16 +239,16 @@
     rows = toks * heads
     half = toks // 2
     flat = lambda x: x.reshape(rows, width)
-    anywhere = pl.BlockSpec(memory_space=pl.ANY)
-    dq, dk, dv = pl.pallas_call(
+    anywhere = pl.BlockSpec(memory_space=pltpu.HBM)
+    in_vmem = pl.BlockSpec(memory_space=pltpu.VMEM)
+    dq, dkv = pl.pallas_call(
         functools.partial(kernel, n, heads),
         out_shape=(
-            jax.ShapeDtypeStruct((rows, width), BF16),
-            jax.ShapeDtypeStruct((toks, width), BF16),
-            jax.ShapeDtypeStruct((toks, width), BF16),
+            pltpu.VMEM((rows, width), BF16),
+            pltpu.VMEM((2, toks, width), BF16),
         ),
         in_specs=[anywhere] * 6 + [pl.BlockSpec(memory_space=pltpu.SMEM)],
-        out_specs=(anywhere,) * 3,
+        out_specs=(in_vmem,) * 2,
         scratch_shapes=[
             pltpu.VMEM((2, rows, width), BF16),
             pltpu.VMEM((2, rows, width), BF16),
@@ -264,7 +262,6 @@
             pltpu.VMEM((n, 2, half, width), BF16),
             pltpu.VMEM((rows, width), F32),
             pltpu.VMEM((rows, width), F32),
-            pltpu.VMEM((rows, width), BF16),
             pltpu.VMEM((2, 2, half, width), BF16),
             pltpu.SemaphoreType.DMA((6,)),
             pltpu.SemaphoreType.DMA((6,)),
@@ -273,9 +270,10 @@
             pltpu.SemaphoreType.DMA((n,)),
             pltpu.SemaphoreType.DMA((n,)),
             pltpu.SemaphoreType.DMA((n,)),
-            pltpu.SemaphoreType.DMA((5,)),
         ],
-        compiler_params=pltpu.CompilerParams(collective_id=0, has_side_effects=True),
+        compiler_params=pltpu.CompilerParams(
+            collective_id=0, has_side_effects=True, vmem_limit_bytes=24 * 2**20
+        ),
     )(
         flat(queries),
         keys[0],
@@ -285,6 +283,18 @@
         flat(d_out),
         span_order[0],
     )
+    dq, dk, dv = pl.pallas_call(
+        store_kernel,
+        out_shape=(
+            jax.ShapeDtypeStruct((rows, width), BF16),
+            jax.ShapeDtypeStruct((toks, width), BF16),
+            jax.ShapeDtypeStruct((toks, width), BF16),
+        ),
+        in_specs=[in_vmem] * 2,
+        out_specs=(anywhere,) * 3,
+        scratch_shapes=[pltpu.SemaphoreType.DMA((3,))],
+        compiler_params=pltpu.CompilerParams(vmem_limit_bytes=4 * 2**20),
+    )(dq, dkv)
     return dq.reshape(queries.shape), dk[None], dv[None]
 
 

time: 20.3 us -> 22.3 us (1.099)
  the two profiles are of different devices: /device:TPU:1 before, /device:TPU:0 now
where the time goes in v2:
time: 22.3 us; the launch traced here: 22 us
  Pallas kernels  16.4 us (74%)
  local copies, waits for them, and re-layouts  4.9 us (22%)
  between operations  0.66 us (3%)
    pallas_call x1, Pallas kernels, body(): pl.pallas_call(functools.partial(kernel, n, heads), out_shape=(pltpu.VMEM...  15.7 us
    unnamed x14, local copies, waits for them, and re-layouts  4.9 us
    pallas_call x1, Pallas kernels, body(): pl.pallas_call(store_kernel, out_shape=(jax.ShapeDtypeStruct((rows, width...  0.7 us

profile of v2, /device:TPU:0, one launch (start us, length us, event | category | flops | bytes accessed | tf_op | source)
XLA Modules:
  0.0 22.0 jit_solution(4436104599607671366)
XLA Ops:
  0.6 0.0 copy-start.5
  0.6 0.0 copy-start.6
  0.7 0.7 %copy-done.5 = f32[1,4,128]{2,1,0:T(4,128)S(1)} copy-done((f32[1,4,128]{2,1,0:T(4,128)S(1)}, f32[1,4,128]{2,1,0:T(4,128)}, u32[]{:S(2)}) %copy-start.5) | copy-done | bytes 2072
  1.3 0.0 copy-done.6
  1.3 0.0 copy-start
  1.3 0.9 %copy-done = bf16[1,128,4,128]{3,2,1,0:T(4,128)(2,1)S(1)} copy-done((bf16[1,128,4,128]{3,2,1,0:T(4,128)(2,1)S(1)}, bf16[1,128,4,128]{3,2,1,0:T(4,128)(2,1)}, u32[]{:S(2)}) %copy-start) | copy-done | bytes 131096
  2.2 0.0 copy-start.1
  2.2 0.9 %copy-done.1 = bf16[1,128,4,128]{3,2,1,0:T(4,128)(2,1)S(1)} copy-done((bf16[1,128,4,128]{3,2,1,0:T(4,128)(2,1)S(1)}, bf16[1,128,4,128]{3,2,1,0:T(4,128)(2,1)}, u32[]{:S(2)}) %copy-start.1) | copy-done | bytes 131096
  3.1 0.0 copy-start.2
  3.1 0.9 %copy-done.2 = bf16[1,128,4,128]{3,2,1,0:T(4,128)(2,1)S(1)} copy-done((bf16[1,128,4,128]{3,2,1,0:T(4,128)(2,1)S(1)}, bf16[1,128,4,128]{3,2,1,0:T(4,128)(2,1)}, u32[]{:S(2)}) %copy-start.2) | copy-done | bytes 131096
  4.0 0.0 copy-start.3
  4.0 0.8 %copy-done.3 = bf16[1,128,128]{2,1,0:T(8,128)(2,1)S(1)} copy-done((bf16[1,128,128]{2,1,0:T(8,128)(2,1)S(1)}, bf16[1,128,128]{2,1,0:T(8,128)(2,1)}, u32[]{:S(2)}) %copy-start.3) | copy-done | bytes 32792
  4.8 0.0 copy-start.4
  4.8 0.8 %copy-done.4 = bf16[1,128,128]{2,1,0:T(8,128)(2,1)S(1)} copy-done((bf16[1,128,128]{2,1,0:T(8,128)(2,1)S(1)}, bf16[1,128,128]{2,1,0:T(8,128)(2,1)}, u32[]{:S(2)}) %copy-start.4) | copy-done | bytes 32792
  5.5 15.7 %shard_map.94 = (bf16[512,128]{1,0:T(8,128)(2,1)S(1)}, bf16[2,128,128]{2,1,0:T(8,128)(2,1)S(1)}) custom-call(bf16[512,128]{1,0:T(8,128)(2,1)S(1)} %bitcast.10, bf16[128,128]{1,0:T(8,128)(2,1)S(1)} %bitcast.13, bf16[128,128]{1,0:T(8,128)(2,1)S(1)} %bitcast.14, bf16[512,128]{1,0:T(8,128)(2,1)S(1)} %bitcast.11, f32[4,128]{1,0:T(4,128)S(1)} %bitcast.15, ...), custom_call_target="tpu_custom_call" | custom-call | tf_op jit(solution)/shard_map/pallas_call | solution.py:244
  21.3 0.7 %shard_map.95 = (bf16[512,128]{1,0:T(8,128)(2,1)}, bf16[128,128]{1,0:T(8,128)(2,1)}, bf16[128,128]{1,0:T(8,128)(2,1)}) custom-call(bf16[512,128]{1,0:T(8,128)(2,1)S(1)} %get-tuple-element.8.dq_ref, bf16[2,128,128]{2,1,0:T(8,128)(2,1)S(1)} %get-tuple-element.9.kv_ref), custom_call_target="tpu_custom_call" | custom-call | tf_op jit(solution)/shard_map/pallas_call | solution.py:286
Async XLA Ops:
  0.6 0.7 %copy-start.5 = (f32[1,4,128]{2,1,0:T(4,128)S(1)}, f32[1,4,128]{2,1,0:T(4,128)}, u32[]{:S(2)}) copy-start(f32[1,4,128]{2,1,0:T(4,128)} %param.11) | copy-start | bytes 6148
  0.6 0.7 %copy-start.6 = (s32[1,8]{1,0:T(1,128)S(1)}, s32[1,8]{1,0:T(1,128)}, u32[]{:S(2)}) copy-start(s32[1,8]{1,0:T(1,128)} %param.13) | copy-start | bytes 100
  1.3 0.9 %copy-start = (bf16[1,128,4,128]{3,2,1,0:T(4,128)(2,1)S(1)}, bf16[1,128,4,128]{3,2,1,0:T(4,128)(2,1)}, u32[]{:S(2)}) copy-start(bf16[1,128,4,128]{3,2,1,0:T(4,128)(2,1)} %param.7) | copy-start | bytes 393220
  2.2 0.9 %copy-start.1 = (bf16[1,128,4,128]{3,2,1,0:T(4,128)(2,1)S(1)}, bf16[1,128,4,128]{3,2,1,0:T(4,128)(2,1)}, u32[]{:S(2)}) copy-start(bf16[1,128,4,128]{3,2,1,0:T(4,128)(2,1)} %param.10) | copy-start | bytes 393220
  3.1 0.9 %copy-start.2 = (bf16[1,128,4,128]{3,2,1,0:T(4,128)(2,1)S(1)}, bf16[1,128,4,128]{3,2,1,0:T(4,128)(2,1)}, u32[]{:S(2)}) copy-start(bf16[1,128,4,128]{3,2,1,0:T(4,128)(2,1)} %param.12) | copy-start | bytes 393220
  4.0 0.8 %copy-start.3 = (bf16[1,128,128]{2,1,0:T(8,128)(2,1)S(1)}, bf16[1,128,128]{2,1,0:T(8,128)(2,1)}, u32[]{:S(2)}) copy-start(bf16[1,128,128]{2,1,0:T(8,128)(2,1)} %param.8) | copy-start | bytes 98308
  4.8 0.8 %copy-start.4 = (bf16[1,128,128]{2,1,0:T(8,128)(2,1)S(1)}, bf16[1,128,128]{2,1,0:T(8,128)(2,1)}, u32[]{:S(2)}) copy-start(bf16[1,128,128]{2,1,0:T(8,128)(2,1)} %param.9) | copy-start | bytes 98308

commit v3 on v2

--- a/solution.py
+++ b/solution.py
@@ -271,9 +271,7 @@
             pltpu.SemaphoreType.DMA((n,)),
             pltpu.SemaphoreType.DMA((n,)),
         ],
-        compiler_params=pltpu.CompilerParams(
-            collective_id=0, has_side_effects=True, vmem_limit_bytes=24 * 2**20
-        ),
+        compiler_params=pltpu.CompilerParams(collective_id=0, has_side_effects=True),
     )(
         flat(queries),
         keys[0],
@@ -293,7 +291,7 @@
         in_specs=[in_vmem] * 2,
         out_specs=(anywhere,) * 3,
         scratch_shapes=[pltpu.SemaphoreType.DMA((3,))],
-        compiler_params=pltpu.CompilerParams(vmem_limit_bytes=4 * 2**20),
+        compiler_params=pltpu.CompilerParams(vmem_limit_bytes=2**20),
     )(dq, dkv)
     return dq.reshape(queries.shape), dk[None], dv[None]
 

time: 22.3 us -> 17.4 us (0.78)
  local copies, waits for them, and re-layouts: 4.9 us -> 0 us
    unnamed x14 -> x0, local copies, waits for them, and re-layouts: 4.9 us -> none
where the time goes in v3:
time: 17.4 us; the launch traced here: 17.2 us
  Pallas kernels  16.5 us (95%)
  between operations  0.64 us (4%)
    pallas_call x1, Pallas kernels, body(): pl.pallas_call(functools.partial(kernel, n, heads), out_shape=(pltpu.VMEM...  15.8 us
    pallas_call x1, Pallas kernels, body(): pl.pallas_call(store_kernel, out_shape=(jax.ShapeDtypeStruct((rows, width...  0.7 us

profile of v3, /device:TPU:0, one launch (start us, length us, event | category | flops | bytes accessed | tf_op | source)
XLA Modules:
  0.0 17.2 jit_solution(17690778668564075517)
XLA Ops:
  0.6 15.8 %shard_map.94 = (bf16[512,128]{1,0:T(8,128)(2,1)S(1)}, bf16[2,128,128]{2,1,0:T(8,128)(2,1)S(1)}) custom-call(bf16[512,128]{1,0:T(8,128)(2,1)} %bitcast.10, bf16[128,128]{1,0:T(8,128)(2,1)} %bitcast.13, bf16[128,128]{1,0:T(8,128)(2,1)} %bitcast.14, bf16[512,128]{1,0:T(8,128)(2,1)} %bitcast.11, f32[4,128]{1,0:T(4,128)} %bitcast.15, bf16[512,128]{1,0:T(8,128)(2,1)} %bitcast.12, ...), custom_call_target="tpu_custom_call" | custom-call | tf_op jit(solution)/shard_map/pallas_call | solution.py:244
  16.5 0.7 %shard_map.95 = (bf16[512,128]{1,0:T(8,128)(2,1)}, bf16[128,128]{1,0:T(8,128)(2,1)}, bf16[128,128]{1,0:T(8,128)(2,1)}) custom-call(bf16[512,128]{1,0:T(8,128)(2,1)S(1)} %get-tuple-element.8.dq_ref, bf16[2,128,128]{2,1,0:T(8,128)(2,1)S(1)} %get-tuple-element.9.kv_ref), custom_call_target="tpu_custom_call" | custom-call | tf_op jit(solution)/shard_map/pallas_call | solution.py:284

commit v4 on v3

--- a/solution.py
+++ b/solution.py
@@ -29,7 +29,7 @@
     o_hbm,
     l_hbm,
     g_hbm,
-    order,
+    order_hbm,
     dq_ref,
     kv_ref,
     qs,
@@ -45,6 +45,7 @@
     dq_send,
     dq_recv,
     fin,
+    order,
     load_sem,
     pair_send,
     pair_recv,
@@ -81,6 +82,7 @@
                 (g_hbm, gs.at[0]),
                 (o_hbm, os_.at[0]),
                 (l_hbm, ls.at[0]),
+                (order_hbm, order),
             )
         )
     ]
@@ -142,6 +144,7 @@
         copy.wait_recv()
     stats(1)
 
+    loads[6].wait()
     tok = (lax.broadcasted_iota(jnp.int32, (1, rows), 1)) // heads
     span = jnp.where(tok < half, order[2 * me], order[2 * me + 1])
     q_pos = span * half + tok % half
@@ -247,7 +250,7 @@
             pltpu.VMEM((rows, width), BF16),
             pltpu.VMEM((2, toks, width), BF16),
         ),
-        in_specs=[anywhere] * 6 + [pl.BlockSpec(memory_space=pltpu.SMEM)],
+        in_specs=[anywhere] * 7,
         out_specs=(in_vmem,) * 2,
         scratch_shapes=[
             pltpu.VMEM((2, rows, width), BF16),
@@ -263,7 +266,8 @@
             pltpu.VMEM((rows, width), F32),
             pltpu.VMEM((rows, width), F32),
             pltpu.VMEM((2, 2, half, width), BF16),
-            pltpu.SemaphoreType.DMA((6,)),
+            pltpu.SMEM((span_order.shape[1],), jnp.int32),
+            pltpu.SemaphoreType.DMA((7,)),
             pltpu.SemaphoreType.DMA((6,)),
             pltpu.SemaphoreType.DMA((6,)),
             pltpu.SemaphoreType.DMA((n,)),

time: 17.4 us -> 16.8 us (0.966)
  Pallas kernels: 16.5 us -> 15.9 us
    pallas_call x1, Pallas kernels: 15.8 us -> 15.2 us  [body(): pl.pallas_call(functools.partial(kernel, n, heads), out_shape=(pltpu.VMEM...]
where the time goes in v4:
time: 16.8 us; the launch traced here: 16.5 us
  Pallas kernels  15.9 us (95%)
  between operations  0.64 us (4%)
    pallas_call x1, Pallas kernels, body(): pl.pallas_call(functools.partial(kernel, n, heads), out_shape=(pltpu.VMEM...  15.2 us
    pallas_call x1, Pallas kernels, body(): pl.pallas_call(store_kernel, out_shape=(jax.ShapeDtypeStruct((rows, width...  0.7 us

profile of v4, /device:TPU:0, one launch (start us, length us, event | category | flops | bytes accessed | tf_op | source)
XLA Modules:
  0.0 16.5 jit_solution(6995775672705263448)
XLA Ops:
  0.6 15.2 %shard_map.94 = (bf16[512,128]{1,0:T(8,128)(2,1)S(1)}, bf16[2,128,128]{2,1,0:T(8,128)(2,1)S(1)}) custom-call(bf16[512,128]{1,0:T(8,128)(2,1)} %bitcast.10, bf16[128,128]{1,0:T(8,128)(2,1)} %bitcast.13, bf16[128,128]{1,0:T(8,128)(2,1)} %bitcast.14, bf16[512,128]{1,0:T(8,128)(2,1)} %bitcast.11, f32[4,128]{1,0:T(4,128)} %bitcast.15, bf16[512,128]{1,0:T(8,128)(2,1)} %bitcast.12, ...), custom_call_target="tpu_custom_call" | custom-call | tf_op jit(solution)/shard_map/pallas_call | solution.py:247
  15.8 0.7 %shard_map.95 = (bf16[512,128]{1,0:T(8,128)(2,1)}, bf16[128,128]{1,0:T(8,128)(2,1)}, bf16[128,128]{1,0:T(8,128)(2,1)}) custom-call(bf16[512,128]{1,0:T(8,128)(2,1)S(1)} %get-tuple-element.8.dq_ref, bf16[2,128,128]{2,1,0:T(8,128)(2,1)S(1)} %get-tuple-element.9.kv_ref), custom_call_target="tpu_custom_call" | custom-call | tf_op jit(solution)/shard_map/pallas_call | solution.py:288

commit v5 on v4

--- a/solution.py
+++ b/solution.py
@@ -66,7 +66,8 @@
         return {"inner": lax.rem(me + d, n)}
 
     barrier = pltpu.get_barrier_semaphore()
-    for d in range(1, n):
+    near = sorted(range(1, n), key=lambda d: (-min(d, n - d), d))
+    for d in near:
         pl.semaphore_signal(barrier, inc=1, device_id=at(d), device_id_type=MESH)
     pl.semaphore_signal(barrier, inc=1, device_id=partner, device_id_type=MESH)
 
@@ -92,7 +93,6 @@
     loads[0].wait()
     loads[1].wait()
     pl.semaphore_wait(barrier, n)
-    near = sorted(range(1, n), key=lambda d: (-min(d, n - d), d))
     kv_copies = {}
     for d in near:
         kv_copies[d] = pltpu.make_async_remote_copy(
@@ -164,24 +164,25 @@
         )
         grad_scores = (probs * (grad_probs - stat[1:2, :]) * scale).astype(BF16)
         ds_all[d] = grad_scores
-        return dot(grad_scores, queries), dot(probs.astype(BF16), grads)
-
-    part[0], part[1] = block(0)
+        yield 1, dot(probs.astype(BF16), grads)
+        yield 0, dot(grad_scores, queries)
+
+    for i, grad in block(0):
+        part[i] = grad
     grad_copies = {}
     for d in reversed(near):
         kv_copies[d].wait_recv()
-        key_grad, value_grad = block(d)
-        send_buf[d, 0] = key_grad.astype(BF16)
-        send_buf[d, 1] = value_grad.astype(BF16)
-        grad_copies[d] = pltpu.make_async_remote_copy(
-            src_ref=send_buf.at[d],
-            dst_ref=recv_buf.at[d],
-            send_sem=grad_send.at[d],
-            recv_sem=grad_recv.at[d],
-            device_id=at(n - d),
-            device_id_type=MESH,
-        )
-        grad_copies[d].start()
+        for i, grad in block(d):
+            send_buf[d, i] = grad.astype(BF16)
+            grad_copies[d, i] = pltpu.make_async_remote_copy(
+                src_ref=send_buf.at[d, i],
+                dst_ref=recv_buf.at[d, i],
+                send_sem=grad_send.at[d, i],
+                recv_sem=grad_recv.at[d, i],
+                device_id=at(n - d),
+                device_id_type=MESH,
+            )
+            grad_copies[d, i].start()
 
     def query_grad(i):
         total = None
@@ -204,27 +205,32 @@
     dq_copy.wait_recv()
     dq_ref[...] = (own_grad + dq_recv[...]).astype(BF16)
 
-    total = part[...]
-    for d in reversed(near):
-        grad_copies[d].wait_recv()
-        total = total + recv_buf[d].astype(F32)
-    fin[0] = total.astype(BF16)
-    fin_copy = pltpu.make_async_remote_copy(
-        src_ref=fin.at[0],
-        dst_ref=fin.at[1],
-        send_sem=pair_send.at[5],
-        recv_sem=pair_recv.at[5],
-        device_id=partner,
-        device_id_type=MESH,
-    )
-    fin_copy.start()
+    fin_copies = []
+    for i in (1, 0):
+        total = part[i]
+        for d in reversed(near):
+            grad_copies[d, i].wait_recv()
+            total = total + recv_buf[d, i].astype(F32)
+        fin[0, i] = total.astype(BF16)
+        copy = pltpu.make_async_remote_copy(
+            src_ref=fin.at[0, i],
+            dst_ref=fin.at[1, i],
+            send_sem=pair_send.at[5 + i],
+            recv_sem=pair_recv.at[5 + i],
+            device_id=partner,
+            device_id_type=MESH,
+        )
+        copy.start()
+        fin_copies.append(copy)
     kv_ref[:, mine] = fin[0]
-    fin_copy.wait_recv()
+    for copy in fin_copies:
+        copy.wait_recv()
     kv_ref[:, theirs] = fin[1]
     for d in near:
         kv_copies[d].wait_send()
-        grad_copies[d].wait_send()
-    for copy in pair_copies + [dq_copy, fin_copy]:
+        grad_copies[d, 0].wait_send()
+        grad_copies[d, 1].wait_send()
+    for copy in pair_copies + [dq_copy] + fin_copies:
         copy.wait_send()
 
 
@@ -268,12 +274,12 @@
             pltpu.VMEM((2, 2, half, width), BF16),
             pltpu.SMEM((span_order.shape[1],), jnp.int32),
             pltpu.SemaphoreType.DMA((7,)),
-            pltpu.SemaphoreType.DMA((6,)),
-            pltpu.SemaphoreType.DMA((6,)),
+            pltpu.SemaphoreType.DMA((7,)),
+            pltpu.SemaphoreType.DMA((7,)),
             pltpu.SemaphoreType.DMA((n,)),
             pltpu.SemaphoreType.DMA((n,)),
-            pltpu.SemaphoreType.DMA((n,)),
-            pltpu.SemaphoreType.DMA((n,)),
+            pltpu.SemaphoreType.DMA((n, 2)),
+            pltpu.SemaphoreType.DMA((n, 2)),
         ],
         compiler_params=pltpu.CompilerParams(collective_id=0, has_side_effects=True),
     )(

time: 16.8 us -> 16.7 us (level)
  no operation moved by 1% of the time
where the time goes in v5:
time: 16.7 us; the launch traced here: 16.5 us
  Pallas kernels  15.8 us (95%)
  between operations  0.64 us (4%)
    pallas_call x1, Pallas kernels, body(): pl.pallas_call(functools.partial(kernel, n, heads), out_shape=(pltpu.VMEM...  15.1 us
    pallas_call x1, Pallas kernels, body(): pl.pallas_call(store_kernel, out_shape=(jax.ShapeDtypeStruct((rows, width...  0.7 us

profile of v5, /device:TPU:0, one launch (start us, length us, event | category | flops | bytes accessed | tf_op | source)
XLA Modules:
  0.0 16.5 jit_solution(1634863334346200752)
XLA Ops:
  0.6 15.1 %shard_map.94 = (bf16[512,128]{1,0:T(8,128)(2,1)S(1)}, bf16[2,128,128]{2,1,0:T(8,128)(2,1)S(1)}) custom-call(bf16[512,128]{1,0:T(8,128)(2,1)} %bitcast.10, bf16[128,128]{1,0:T(8,128)(2,1)} %bitcast.13, bf16[128,128]{1,0:T(8,128)(2,1)} %bitcast.14, bf16[512,128]{1,0:T(8,128)(2,1)} %bitcast.11, f32[4,128]{1,0:T(4,128)} %bitcast.15, bf16[512,128]{1,0:T(8,128)(2,1)} %bitcast.12, ...), custom_call_target="tpu_custom_call" | custom-call | tf_op jit(solution)/shard_map/pallas_call | solution.py:253
  15.8 0.7 %shard_map.95 = (bf16[512,128]{1,0:T(8,128)(2,1)}, bf16[128,128]{1,0:T(8,128)(2,1)}, bf16[128,128]{1,0:T(8,128)(2,1)}) custom-call(bf16[512,128]{1,0:T(8,128)(2,1)S(1)} %get-tuple-element.8.dq_ref, bf16[2,128,128]{2,1,0:T(8,128)(2,1)S(1)} %get-tuple-element.9.kv_ref), custom_call_target="tpu_custom_call" | custom-call | tf_op jit(solution)/shard_map/pallas_call | solution.py:294
